TPU v7x, 256 devices: a whole 4x4x8 slice. The times are simulated.
256 devices in a mesh: batch: 8 (over x, core), cache: 32 (over y, z).
Axes of the slice: x: 4, y: 4, z: 8, core: 2. Of those that a mesh axis runs over, the one named last changes fastest.
Arguments:
- hidden_in: bfloat16 [64, 4096], P('batch'), may hold values from -6 to 6
- attn_gain: bfloat16 [4096], replicated, may hold values from 0.25 to 1.75
- w_query: bfloat16 [4096, 4096], P(None, 'cache'), may hold values from -0.09375 to 0.09375
- w_key: bfloat16 [4096, 1024], P(None, 'cache'), may hold values from -0.09375 to 0.09375
- w_value: bfloat16 [4096, 1024], P(None, 'cache'), may hold values from -0.09375 to 0.09375
- key_cache: bfloat16 [64, 4096, 1024], P('batch', 'cache'), may hold values from -400 to 400, as said below
- value_cache: bfloat16 [64, 4096, 1024], P('batch', 'cache'), may hold values from -6 to 6
- write_pos: int32 [64], P('batch'), may hold values from 0 to 12287, as said below
- cache_len: int32 [64], P('batch'), may hold values from 0 to 4095, as said below
- w_out: bfloat16 [4096, 4096], P('cache'), may hold values from -0.1875 to 0.1875
- mlp_gain: bfloat16 [4096], replicated, may hold values from 0.25 to 1.75
- w_gate: bfloat16 [4096, 7168], P(None, 'cache'), may hold values from -0.09375 to 0.09375
- w_up: bfloat16 [4096, 7168], P(None, 'cache'), may hold values from -0.09375 to 0.09375
- w_down: bfloat16 [7168, 4096], P('cache'), may hold values from -0.125 to 0.125
Outputs:
- hidden_out: bfloat16 [64, 4096], P('batch', 'cache')
Inputs may be any that keep to these rules, and one draw needn't show every extreme that they name: `key_cache`: keys of earlier tokens are finite reals. `write_pos`: positions of the new tokens; the largest value occurs in every draw. cache_len never exceeds write_pos; both 0 and 4095 occur in every draw, and many sequences attend fewer than 4095 earlier tokens.
All inputs are finite; a program needn't handle non-finite values.
Results may differ from a plain program's by a relative error of at most 0.017.
Values may be sent and summed in bfloat16 or wider, within the bound.
A program may use at most 64 MiB of HBM per device.

v0:
```python
import jax
import jax.numpy as jnp
from jax import lax
from jax.sharding import PartitionSpec as P

HEADS = 32
KV_HEADS = 8
HEAD_DIM = 128


def sent_together(arrays, axis, dim, along):
    widths = [a.shape[along] for a in arrays]
    both = jnp.concatenate(arrays, axis=along)
    out = lax.all_gather(both, axis, axis=dim, tiled=True)
    return tuple(jnp.split(out, [sum(widths[:k]) for k in range(1, len(widths))], axis=along))


def sent_to_all(x, axis):
    copies = jnp.broadcast_to(x, (lax.axis_size(axis), *x.shape))
    return lax.all_to_all(copies, axis, split_axis=0, concat_axis=0, tiled=True)


def of_everyone(x, axis):
    return sent_to_all(x, axis).max(axis=0)


def over_copies(x, axis):
    return sent_to_all(x, axis).sum(axis=0)


def cut_along(x, dim, devices):
    before, after = (x.shape[:dim], x.shape[dim + 1 :])
    return jnp.moveaxis(x.reshape(*before, devices, -1, *after), dim, 0)


def sum_at_owner(x, axis, dim):
    devices = lax.axis_size(axis)
    parts = lax.all_to_all(cut_along(x, dim, devices), axis, 0, 0, tiled=True)
    return jnp.sum(parts.astype(jnp.float32), axis=0)


def laid_out(parts, dim):
    parts = jnp.moveaxis(parts, 0, dim)
    lengths = parts.shape
    return parts.reshape(*lengths[:dim], lengths[dim] * lengths[dim + 1], *lengths[dim + 2 :])


def gather_directly(x, axis, dim):
    parts = sent_to_all(x, axis)
    return laid_out(parts, dim)


def rms_norm(values, gain):
    wide = values.astype(jnp.float32)
    spread = jnp.mean(wide * wide, axis=-1, keepdims=True)
    return (wide * lax.rsqrt(spread + 1e-05) * gain.astype(jnp.float32)).astype(jnp.bfloat16)


def rotate(heads, position):
    half = heads.shape[-1] // 2
    freq = 10000.0 ** (-(jnp.arange(half, dtype=jnp.float32) * 2.0 / heads.shape[-1]))
    angle = position.astype(jnp.float32)[:, None] * freq[None, :]
    cosine = jnp.cos(angle)[:, None, :]
    sine = jnp.sin(angle)[:, None, :]
    first = heads[..., :half]
    second = heads[..., half:]
    return jnp.concatenate(
        [first * cosine - second * sine, second * cosine + first * sine], axis=-1
    )


def per_device(
    hidden_in,
    attn_gain,
    w_query,
    w_key,
    w_value,
    key_cache,
    value_cache,
    write_pos,
    cache_len,
    w_out,
    mlp_gain,
    w_gate,
    w_up,
    w_down,
):
    seqs = hidden_in.shape[0]
    embedding_width = hidden_in.shape[1]
    ncache = lax.axis_size("cache")
    position_index = lax.axis_index("cache")
    slots_dev = key_cache.shape[1]
    window = slots_dev * ncache
    group = HEADS // KV_HEADS
    scale = 1.0 / HEAD_DIM**0.5
    feature_width = embedding_width // ncache
    normed = rms_norm(hidden_in, attn_gain)
    query_slice = jnp.dot(normed, w_query, preferred_element_type=jnp.float32).astype(jnp.bfloat16)
    key_part = jnp.dot(normed, w_key, preferred_element_type=jnp.float32).astype(jnp.bfloat16)
    value_part = jnp.dot(normed, w_value, preferred_element_type=jnp.float32).astype(jnp.bfloat16)
    query_raw, key_raw, value_new = (
        lax.all_gather(query_slice, "cache", axis=1, tiled=True),
        *sent_together((key_part, value_part), "cache", 1, 0),
    )
    query = rotate(query_raw.astype(jnp.float32).reshape(seqs, HEADS, HEAD_DIM), write_pos).astype(
        jnp.bfloat16
    )
    fresh_key_row = rotate(
        key_raw.astype(jnp.float32).reshape(seqs, KV_HEADS, HEAD_DIM), write_pos
    ).astype(jnp.bfloat16)
    value_heads = value_new.reshape(seqs, KV_HEADS, HEAD_DIM)
    slots = position_index * slots_dev + jnp.arange(slots_dev, dtype=jnp.int32)
    dist = (write_pos[:, None] - 1 - slots[None, :]) % window + 1
    valid = dist <= cache_len[:, None]
    owner = write_pos % window // slots_dev == position_index
    query_head_group = query.reshape(seqs, KV_HEADS, group, HEAD_DIM)
    keys = key_cache.reshape(seqs, slots_dev, KV_HEADS, HEAD_DIM)
    values = value_cache.reshape(seqs, slots_dev, KV_HEADS, HEAD_DIM)
    scores = (
        jnp.einsum("bkgd,bwkd->bkgw", query_head_group, keys, preferred_element_type=jnp.float32)
        * scale
    )
    own = (
        jnp.einsum(
            "vyjf,vyf->vyj", query_head_group, fresh_key_row, preferred_element_type=jnp.float32
        )
        * scale
    )
    scores = jnp.where(valid[:, None, None, :], scores, -1e30)
    own = jnp.where(owner[:, None, None], own, -1e30)
    top = jnp.maximum(jnp.max(scores, axis=-1), own)
    weights = jnp.where(valid[:, None, None, :], jnp.exp(scores - top[..., None]), 0.0)
    own_weight = jnp.where(owner[:, None, None], jnp.exp(own - top), 0.0)
    total = jnp.sum(weights, axis=-1) + own_weight
    own_low = lax.optimization_barrier(own_weight.astype(jnp.bfloat16)).astype(jnp.float32)
    reduced_total = jnp.einsum(
        "bkgw,bwkd->bkgd", weights.astype(jnp.bfloat16), values, preferred_element_type=jnp.float32
    )
    reduced_total = (
        reduced_total + own_low[..., None] * value_heads.astype(jnp.float32)[:, :, None, :]
    )
    top_flat = top.reshape(seqs, HEADS)
    total_flat = total.reshape(seqs, HEADS)
    summed_flat = reduced_total.reshape(seqs, HEADS, HEAD_DIM)
    largest = of_everyone(top_flat, "cache")
    factor = jnp.exp(top_flat - largest)
    scaled_total = over_copies(total_flat * factor, "cache")
    scaled_sum = (summed_flat * factor[..., None]).reshape(seqs, HEADS * HEAD_DIM)
    local_partial_sum = sum_at_owner(scaled_sum.astype(jnp.bfloat16), "cache", 1)
    total_features = jnp.repeat(scaled_total, HEAD_DIM, axis=1)
    own_total = lax.dynamic_slice_in_dim(
        total_features, position_index * feature_width, feature_width, 1
    )
    attended = (local_partial_sum / own_total).astype(jnp.bfloat16)
    projected = jnp.dot(attended, w_out, preferred_element_type=jnp.float32)
    share = sum_at_owner(projected.astype(jnp.bfloat16), "cache", 1)
    hidden_share = lax.dynamic_slice_in_dim(
        hidden_in, position_index * feature_width, feature_width, 1
    )
    mid_own = (hidden_share.astype(jnp.float32) + share).astype(jnp.bfloat16)
    mid_wide = mid_own.astype(jnp.float32)
    squares = over_copies(jnp.sum(mid_wide * mid_wide, axis=-1), "cache")
    gain_share = lax.dynamic_slice_in_dim(
        mlp_gain, position_index * feature_width, feature_width, 0
    )
    normed_share = (
        mid_wide
        * lax.rsqrt(squares / embedding_width + 1e-05)[:, None]
        * gain_share.astype(jnp.float32)
    ).astype(jnp.bfloat16)
    normed_mid = gather_directly(normed_share, "cache", 1)
    gate = jnp.dot(normed_mid, w_gate, preferred_element_type=jnp.float32)
    upper = jnp.dot(normed_mid, w_up, preferred_element_type=jnp.float32)
    act = (jax.nn.silu(gate) * upper).astype(jnp.bfloat16)
    down = jnp.dot(act, w_down, preferred_element_type=jnp.float32)
    down_own = sum_at_owner(down.astype(jnp.bfloat16), "cache", 1)
    return (mid_own.astype(jnp.float32) + down_own).astype(jnp.bfloat16)


def solution(mesh):
    in_specs = (
        P("batch", None),
        P(),
        P(None, "cache"),
        P(None, "cache"),
        P(None, "cache"),
        P("batch", "cache", None),
        P("batch", "cache", None),
        P("batch"),
        P("batch"),
        P("cache", None),
        P(),
        P(None, "cache"),
        P(None, "cache"),
        P("cache", None),
    )
    out_specs = P("batch", "cache")
    return jax.shard_map(
        per_device, mesh=mesh, in_specs=in_specs, out_specs=out_specs, check_vma=False
    )
```

profile of v0, /device:TPU:4, one launch (start us, length us, event | category | flops | bytes accessed | tf_op | source)
XLA Modules:
  0.0 211.6 jit_solution(16157100261924183315)
XLA Ops:
  0.0 0.0 copy-start
  0.0 0.0 copy-start.2
  0.0 0.8 fusion.62
  0.8 0.7 fusion.52
  1.5 1.0 fusion.18
  2.5 0.7 convert_element_type.92
  3.2 1.2 convolution_convert_fusion.3
  4.5 1.2 convolution_convert_fusion.2
  5.7 1.6 convolution_convert_fusion.4
  7.3 52.3 %all_gather.6 = bf16[8,4096]{1,0:T(8,128)(2,1)S(1)} all-gather(bf16[8,128]{1,0:T(8,128)(2,1)S(1)} %convolution_convert_fusion.4), channel_id=1, replica_groups=mesh['batch'=8,'cache'=32] {'cache'}, dimensions={1}, use_global_device_ids=true | all-gather | bytes 67584 | tf_op jit(solution)/shard_map/all_gather | solution.py:102
  59.6 0.1 multiply_cosine_fusion
  59.7 0.1 subtract_convert_fusion
  59.9 42.2 %all-gather = bf16[32,32,16]{1,2,0:T(8,128)(2,1)S(1)} all-gather(bf16[1,32,16]{1,2,0:T(8,128)(2,1)S(1)} %maximum_bitcast_fusion.1), channel_id=1, replica_groups=mesh['batch'=8,'cache'=32] {'cache'}, dimensions={0}, use_global_device_ids=true | all-gather | bytes 33792 | tf_op jit(solution)/shard_map/all_gather | solution.py:14
  102.2 0.2 reshape.209
  102.4 0.1 subtract_convert_fusion.1
  102.4 0.1 maximum_bitcast_fusion
  102.5 0.0 copy-done.2
  102.5 0.1 fusion.44
  102.6 0.3 fusion.33
  102.9 0.0 copy-done
  102.9 1.3 fusion.63
  104.2 0.1 fusion.35
  104.3 0.1 copy.61
  104.4 0.1 copy.63
  104.5 0.7 reshape.212
  105.2 5.7 %all-to-all-start = ((f32[32,1,256]{2,1,0:T(1,128)}), f32[32,1,256]{2,1,0:T(1,128)S(1)}, u32[]{:S(2)}, u32[]{:S(2)}) async-start(f32[32,1,256]{2,1,0:T(1,128)} %reshape.212), calls=%async_computation | async-start | bytes 65536 | tf_op jit(solution)/shard_map/all_to_all | solution.py:20
  110.9 0.3 fusion.22
  111.2 0.1 fusion.56
  111.3 0.0 copy-start.1
  111.3 2.4 %fusion.12 = f32[8,8,4,128]{3,2,1,0:T(4,128)S(1)} fusion(f32[8,8,4,128]{3,2,1,0:T(4,128)S(1)} %get-tuple-element.22, f32[8,8,128]{2,1,0:T(8,128)S(1)} %copy.60, f32[8,8,4]{2,1,0:T(8,128)S(1)} %convert_element_type.100, f32[8,8,4]{2,1,0:T(8,128)S(1)} %fusion.35, pred[8,128]{1,0:T(8,128)(4,1)S(1)} %fusion.44, bf16[8,128,1024]{2,1,0:T(8,128)(2,1)} %param.20), kind=kOutput, calls=%fused_computation.10 | convolution fusion | flops 8552448 | bytes 2395136 | tf_op jit(solution)/shard_map/bkgw,bwkd->bkgd/dot_general | solution.py:136
  113.7 0.1 copy.66
  113.8 0.1 copy.67
  113.9 6.9 %all-to-all-done = f32[32,1,256]{2,1,0:T(1,128)S(1)} async-done(((f32[32,1,256]{2,1,0:T(1,128)}), f32[32,1,256]{2,1,0:T(1,128)S(1)}, u32[]{:S(2)}, u32[]{:S(2)}) %all-to-all-start) | async-done | bytes 32800 | tf_op jit(solution)/shard_map/all_to_all | solution.py:20
  120.8 0.5 broadcast.173
  121.4 0.7 reduce.1
  122.1 0.1 reshape.213
  122.2 0.1 copy.64
  122.3 0.7 reshape.214
  123.0 3.8 %all-to-all-start.2 = ((f32[32,1,256]{2,1,0:T(1,128)}), f32[32,1,256]{2,1,0:T(1,128)S(1)}, u32[]{:S(2)}, u32[]{:S(2)}) async-start(f32[32,1,256]{2,1,0:T(1,128)} %reshape.214), calls=%async_computation.2 | async-start | bytes 65536 | tf_op jit(solution)/shard_map/all_to_all | solution.py:20
  126.8 0.7 fusion.25
  127.6 9.1 %all-to-all-done.2 = f32[32,1,256]{2,1,0:T(1,128)S(1)} async-done(((f32[32,1,256]{2,1,0:T(1,128)}), f32[32,1,256]{2,1,0:T(1,128)S(1)}, u32[]{:S(2)}, u32[]{:S(2)}) %all-to-all-start.2) | async-done | bytes 32800 | tf_op jit(solution)/shard_map/all_to_all | solution.py:20
  136.7 3.9 %all-to-all-start.1 = ((bf16[32,8,128]{2,1,0:T(8,128)(2,1)}), bf16[32,8,128]{2,1,0:T(8,128)(2,1)S(1)}, u32[]{:S(2)}, u32[]{:S(2)}) async-start(bf16[32,8,128]{2,1,0:T(8,128)(2,1)} %fusion.25), calls=%async_computation.1 | async-start | bytes 131072 | tf_op jit(solution)/shard_map/all_to_all | solution.py:38
  140.6 0.7 reduce.2
  141.3 0.1 reshape.215
  141.4 0.1 copy.68
  141.5 0.1 broadcast_bitcast_fusion
  141.6 9.0 %all-to-all-done.1 = bf16[32,8,128]{2,1,0:T(8,128)(2,1)S(1)} async-done(((bf16[32,8,128]{2,1,0:T(8,128)(2,1)}), bf16[32,8,128]{2,1,0:T(8,128)(2,1)S(1)}, u32[]{:S(2)}, u32[]{:S(2)}) %all-to-all-start.1) | async-done | bytes 65568 | tf_op jit(solution)/shard_map/all_to_all | solution.py:38
  150.6 0.0 copy-done.1
  150.6 0.2 fusion.15
  150.9 13.2 %all_to_all.36 = bf16[32,8,128]{2,1,0:T(8,128)(2,1)S(1)} all-to-all(bf16[32,8,128]{2,1,0:T(8,128)(2,1)S(1)} %fusion.15), channel_id=1, replica_groups=mesh['batch'=8,'cache'=32] {'cache'}, dimensions={0} | all-to-all | bytes 131072 | tf_op jit(solution)/shard_map/all_to_all | solution.py:38
  164.1 0.8 fusion.45
  164.9 0.6 broadcast_in_dim.83
  165.5 3.9 %all-to-all-start.4 = ((f32[32,1,8]{2,1,0:T(1,128)}), f32[32,1,8]{2,1,0:T(1,128)S(1)}, u32[]{:S(2)}, u32[]{:S(2)}) async-start(f32[32,1,8]{2,1,0:T(1,128)} %broadcast_in_dim.83), calls=%async_computation.4 | async-start | bytes 32768 | tf_op jit(solution)/shard_map/all_to_all | solution.py:20
  169.3 0.8 dynamic-slice_convert_fusion
  170.1 9.1 %all-to-all-done.4 = f32[32,1,8]{2,1,0:T(1,128)S(1)} async-done(((f32[32,1,8]{2,1,0:T(1,128)}), f32[32,1,8]{2,1,0:T(1,128)S(1)}, u32[]{:S(2)}, u32[]{:S(2)}) %all-to-all-start.4) | async-done | bytes 1056 | tf_op jit(solution)/shard_map/all_to_all | solution.py:20
  179.1 0.1 reduce_sum.78
  179.2 0.1 fusion.47
  179.3 13.0 %all_to_all.37 = bf16[32,8,128]{2,1,0:T(8,128)(2,1)S(1)} all-to-all(bf16[32,8,128]{2,1,0:T(8,128)(2,1)S(1)} %broadcast_in_dim.84), channel_id=1, replica_groups=mesh['batch'=8,'cache'=32] {'cache'}, dimensions={0} | all-to-all | bytes 131072 | tf_op jit(solution)/shard_map/all_to_all | solution.py:20
  192.3 2.1 fusion.28
  194.3 3.4 %fusion.16 = bf16[32,8,128]{2,1,0:T(8,128)(2,1)S(1)} fusion(bf16[224,4096]{1,0:T(8,128)(2,1)} %param.27, bf16[4096,224]{0,1:T(8,128)(2,1)} %param.26, bf16[32,8,128]{2,1,0:T(8,128)(2,1)S(1)} %all_to_all.37, f32[8,224]{1,0:T(8,128)S(1)} %fusion.28), kind=kOutput, calls=%fused_computation.12 | convolution fusion | flops 29403648 | bytes 3808256 | tf_op jit(solution)/shard_map/dot_general | solution.py:175
  197.8 13.2 %all_to_all.38 = bf16[32,8,128]{2,1,0:T(8,128)(2,1)S(1)} all-to-all(bf16[32,8,128]{2,1,0:T(8,128)(2,1)S(1)} %fusion.16), channel_id=1, replica_groups=mesh['batch'=8,'cache'=32] {'cache'}, dimensions={0} | all-to-all | bytes 131072 | tf_op jit(solution)/shard_map/all_to_all | solution.py:38
  211.0 0.6 fusion.48
  (21 shorter events, 0.4 us)
Async XLA Ops:
  0.0 102.9 %copy-start = (bf16[8,128,1024]{2,1,0:T(8,128)(2,1)S(1)}, bf16[8,128,1024]{2,1,0:T(8,128)(2,1)}, u32[]{:S(2)}) copy-start(bf16[8,128,1024]{2,1,0:T(8,128)(2,1)} %param.19) | copy-start | bytes 6291460
  0.0 102.5 %copy-start.2 = (s32[8]{0:T(128)S(1)}, s32[8]{0:T(128)}, u32[]{:S(2)}) copy-start(s32[8]{0:T(128)} %param.22) | copy-start | bytes 100
  105.2 15.6 %all-to-all-start = ((f32[32,1,256]{2,1,0:T(1,128)}), f32[32,1,256]{2,1,0:T(1,128)S(1)}, u32[]{:S(2)}, u32[]{:S(2)}) async-start(f32[32,1,256]{2,1,0:T(1,128)} %reshape.212), calls=%async_computation | async-start | bytes 65536 | tf_op jit(solution)/shard_map/all_to_all | solution.py:20
  111.3 39.3 %copy-start.1 = (bf16[128,4096]{1,0:T(8,128)(2,1)S(1)}, bf16[128,4096]{1,0:T(8,128)(2,1)}, u32[]{:S(2)}) copy-start(bf16[128,4096]{1,0:T(8,128)(2,1)} %param.23) | copy-start | bytes 3145732
  123.0 13.7 %all-to-all-start.2 = ((f32[32,1,256]{2,1,0:T(1,128)}), f32[32,1,256]{2,1,0:T(1,128)S(1)}, u32[]{:S(2)}, u32[]{:S(2)}) async-start(f32[32,1,256]{2,1,0:T(1,128)} %reshape.214), calls=%async_computation.2 | async-start | bytes 65536 | tf_op jit(solution)/shard_map/all_to_all | solution.py:20
  136.7 13.9 %all-to-all-start.1 = ((bf16[32,8,128]{2,1,0:T(8,128)(2,1)}), bf16[32,8,128]{2,1,0:T(8,128)(2,1)S(1)}, u32[]{:S(2)}, u32[]{:S(2)}) async-start(bf16[32,8,128]{2,1,0:T(8,128)(2,1)} %fusion.25), calls=%async_computation.1 | async-start | bytes 131072 | tf_op jit(solution)/shard_map/all_to_all | solution.py:38
  165.5 13.7 %all-to-all-start.4 = ((f32[32,1,8]{2,1,0:T(1,128)}), f32[32,1,8]{2,1,0:T(1,128)S(1)}, u32[]{:S(2)}, u32[]{:S(2)}) async-start(f32[32,1,8]{2,1,0:T(1,128)} %broadcast_in_dim.83), calls=%async_computation.4 | async-start | bytes 32768 | tf_op jit(solution)/shard_map/all_to_all | solution.py:20
where the time goes:
time: 212 us
  blocking collectives  134 us (63%)
  waiting for transfers between devices  34.1 us (16%)
  starting transfers between devices  17.2 us (8%)
  matrix products  13.7 us (6%)
  other arithmetic  8.78 us (4%)
  local copies, waits for them, and re-layouts  3.68 us (2%)
    all_gather x1, blocking collectives, per_device(): lax.all_gather(query_slice, 'cache', axis=1, tiled=True)  52.3 us
    all_gather x1, blocking collectives, sent_together(): out = lax.all_gather(both, axis, axis=dim, tiled=True)  42.2 us
    all_to_all x2, blocking collectives, sum_at_owner(): parts = lax.all_to_all(cut_along(x, dim, devices), axis, 0, 0, tiled=True)  26.3 us
    all_to_all x3, waiting for transfers between devices, sent_to_all(): return lax.all_to_all(copies, axis, split_axis=0, concat_axis=0, tiled=True)  25.1 us
    all_to_all x3, starting transfers between devices, sent_to_all(): return lax.all_to_all(copies, axis, split_axis=0, concat_axis=0, tiled=True)  13.3 us
    all_to_all x1, blocking collectives, sent_to_all(): return lax.all_to_all(copies, axis, split_axis=0, concat_axis=0, tiled=True)  13 us
    all_to_all x1, waiting for transfers between devices, sum_at_owner(): parts = lax.all_to_all(cut_along(x, dim, devices), axis, 0, 0, tiled=True)  8.97 us
  transfers between devices with their start and end apart: 4, of which 4 were waited for; matrix products, arithmetic and copies ran while one was open for 3% of the time, Pallas kernels for 0%

commit v1 on v0

--- a/solution.py
+++ b/solution.py
@@ -6,6 +6,18 @@
 HEADS = 32
 KV_HEADS = 8
 HEAD_DIM = 128
+
+
+def doubled_up(shard, axis, dim):
+    ways, here = (lax.axis_size(axis), lax.axis_index(axis))
+    grown, reach = (shard, 1)
+    while reach < ways:
+        theirs = lax.ppermute(grown, axis, [(d, d ^ reach) for d in range(ways)])
+        mine_first = jnp.concatenate([grown, theirs], axis=dim)
+        theirs_first = jnp.concatenate([theirs, grown], axis=dim)
+        grown = jnp.where(here & reach == 0, mine_first, theirs_first)
+        reach = 2 * reach
+    return grown
 
 
 def sent_together(arrays, axis, dim, along):
@@ -99,7 +111,7 @@
     key_part = jnp.dot(normed, w_key, preferred_element_type=jnp.float32).astype(jnp.bfloat16)
     value_part = jnp.dot(normed, w_value, preferred_element_type=jnp.float32).astype(jnp.bfloat16)
     query_raw, key_raw, value_new = (
-        lax.all_gather(query_slice, "cache", axis=1, tiled=True),
+        doubled_up(query_slice, "cache", 1),
         *sent_together((key_part, value_part), "cache", 1, 0),
     )
     query = rotate(query_raw.astype(jnp.float32).reshape(seqs, HEADS, HEAD_DIM), write_pos).astype(

time: 212 us -> 187 us (0.88)
  blocking collectives: 134 us -> 85 us
  waiting for transfers between devices: 34.1 us -> 47.3 us
  starting transfers between devices: 17.2 us -> 27.5 us
    all_gather x1 -> x0, blocking collectives: 52.3 us -> none  [per_device(): lax.all_gather(query_slice, 'cache', axis=1, tiled=True)]
    ppermute x0 -> x5, waiting for transfers between devices: none -> 12.8 us  [doubled_up(): theirs = lax.ppermute(grown, axis, [(d, d ^ reach) for d in range(ways)])]
    ppermute x0 -> x5, starting transfers between devices: none -> 9.85 us  [doubled_up(): theirs = lax.ppermute(grown, axis, [(d, d ^ reach) for d in range(ways)])]
    all_gather x1, blocking collectives: 42.2 us -> 45.8 us  [sent_together(): out = lax.all_gather(both, axis, axis=dim, tiled=True)]
  transfers between devices with their start and end apart: 4 -> 9, of which waited for: 4 -> 8; matrix products, arithmetic and copies ran while one was open for 3% -> 5% of each run, Pallas kernels for 0% -> 0%
where the time goes in v1:
time: 187 us; the launch traced here: 186 us
  blocking collectives  85 us (45%)
  waiting for transfers between devices  47.3 us (25%)
  starting transfers between devices  27.5 us (15%)
  matrix products  13.7 us (7%)
  other arithmetic  8.26 us (4%)
  local copies, waits for them, and re-layouts  4.28 us (2%)
    all_gather x1, blocking collectives, sent_together(): out = lax.all_gather(both, axis, axis=dim, tiled=True)  45.8 us
    all_to_all x2, blocking collectives, sum_at_owner(): parts = lax.all_to_all(cut_along(x, dim, devices), axis, 0, 0, tiled=True)  26.3 us
    all_to_all x3, waiting for transfers between devices, sent_to_all(): return lax.all_to_all(copies, axis, split_axis=0, concat_axis=0, tiled=True)  25.4 us
    all_to_all x3, starting transfers between devices, sent_to_all(): return lax.all_to_all(copies, axis, split_axis=0, concat_axis=0, tiled=True)  13.8 us
    all_to_all x1, blocking collectives, sent_to_all(): return lax.all_to_all(copies, axis, split_axis=0, concat_axis=0, tiled=True)  13 us
    ppermute x5, waiting for transfers between devices, doubled_up(): theirs = lax.ppermute(grown, axis, [(d, d ^ reach) for d in range(ways)])  12.8 us
    ppermute x5, starting transfers between devices, doubled_up(): theirs = lax.ppermute(grown, axis, [(d, d ^ reach) for d in range(ways)])  9.85 us
    all_to_all x1, waiting for transfers between devices, sum_at_owner(): parts = lax.all_to_all(cut_along(x, dim, devices), axis, 0, 0, tiled=True)  8.97 us
  transfers between devices with their start and end apart: 9, of which 8 were waited for; matrix products, arithmetic and copies ran while one was open for 5% of the time, Pallas kernels for 0%

profile of v1, /device:TPU:4, one launch (start us, length us, event | category | flops | bytes accessed | tf_op | source)
XLA Modules:
  0.0 186.3 jit_solution(11774323800787713188)
XLA Ops:
  0.0 1.2 fusion.18
  1.2 0.7 convert_element_type.95
  1.9 1.6 convolution_convert_fusion.4
  3.4 2.0 %collective-permute-start = (bf16[8,128]{1,0:T(8,128)(2,1)S(1)}, bf16[8,128]{1,0:T(8,128)(2,1)S(1)}, u32[]{:S(2)}, u32[]{:S(2)}) collective-permute-start(bf16[8,128]{1,0:T(8,128)(2,1)S(1)} %convolution_convert_fusion.4), channel_id=1, source_target_pairs={{0,1},{1,0},{2,3},{3,2},{4,5},{5,4},{6,7},{7,6},{8,9},{9,8},{10,11... | collective-permute-start | bytes 6152 | tf_op jit(solution)/shard_map/ppermute | solution.py:15
  5.4 0.7 fusion.63
  6.2 1.2 convolution_convert_fusion.3
  7.4 1.2 convolution_convert_fusion.2
  8.7 45.8 %all-gather = bf16[32,32,16]{1,2,0:T(8,128)(2,1)S(1)} all-gather(bf16[1,32,16]{1,2,0:T(8,128)(2,1)S(1)} %maximum_bitcast_fusion.1), channel_id=1, replica_groups=mesh['batch'=8,'cache'=32] {'cache'}, dimensions={0}, use_global_device_ids=true | all-gather | bytes 33792 | tf_op jit(solution)/shard_map/all_gather | solution.py:26
  54.4 0.2 reshape.216
  54.6 0.1 multiply_cosine_fusion
  54.8 0.1 fusion.45
  54.8 0.1 subtract_convert_fusion.1
  55.0 1.5 collective-permute-start.1
  56.5 0.1 maximum_bitcast_fusion
  56.6 0.6 copy.60
  57.2 2.4 %collective-permute-done.1 = bf16[8,256]{1,0:T(8,128)(2,1)S(1)} collective-permute-done((bf16[8,256]{1,0:T(8,128)(2,1)S(1)}, bf16[8,256]{1,0:T(8,128)(2,1)S(1)}, u32[]{:S(2)}, u32[]{:S(2)}) %collective-permute-start.1) | collective-permute-done | bytes 4128 | tf_op jit(solution)/shard_map/ppermute | solution.py:15
  59.6 3.6 %collective-permute-start.2 = (bf16[8,512]{1,0:T(8,128)(2,1)S(1)}, bf16[8,512]{1,0:T(8,128)(2,1)S(1)}, u32[]{:S(2)}, u32[]{:S(2)}) collective-permute-start(bf16[8,512]{1,0:T(8,128)(2,1)S(1)} %maximum_select_fusion.6), channel_id=1, source_target_pairs={{0,4},{1,5},{2,6},{3,7},{4,0},{5,1},{6,2},{7,3},{8,12},{9,13},{10,... | collective-permute-start | bytes 24584 | tf_op jit(solution)/shard_map/ppermute | solution.py:15
  63.2 4.0 %collective-permute-done.2 = bf16[8,512]{1,0:T(8,128)(2,1)S(1)} collective-permute-done((bf16[8,512]{1,0:T(8,128)(2,1)S(1)}, bf16[8,512]{1,0:T(8,128)(2,1)S(1)}, u32[]{:S(2)}, u32[]{:S(2)}) %collective-permute-start.2) | collective-permute-done | bytes 8224 | tf_op jit(solution)/shard_map/ppermute | solution.py:15
  67.2 1.0 collective-permute-start.3
  68.2 2.7 %collective-permute-done.3 = bf16[8,1024]{1,0:T(8,128)(2,1)S(1)} collective-permute-done((bf16[8,1024]{1,0:T(8,128)(2,1)S(1)}, bf16[8,1024]{1,0:T(8,128)(2,1)S(1)}, u32[]{:S(2)}, u32[]{:S(2)}) %collective-permute-start.3) | collective-permute-done | bytes 16416 | tf_op jit(solution)/shard_map/ppermute | solution.py:15
  70.9 1.7 collective-permute-start.4
  72.6 3.8 %collective-permute-done.4 = bf16[8,2048]{1,0:T(8,128)(2,1)S(1)} collective-permute-done((bf16[8,2048]{1,0:T(8,128)(2,1)S(1)}, bf16[8,2048]{1,0:T(8,128)(2,1)S(1)}, u32[]{:S(2)}, u32[]{:S(2)}) %collective-permute-start.4) | collective-permute-done | bytes 32800 | tf_op jit(solution)/shard_map/ppermute | solution.py:15
  76.4 0.1 subtract_convert_fusion
  76.6 0.3 fusion.34
  76.9 1.3 fusion.64
  78.2 0.1 fusion.36
  78.3 0.1 copy.61
  78.4 0.1 copy.63
  78.5 0.3 fusion.22
  78.8 0.1 fusion.57
  78.9 0.7 reshape.219
  79.6 6.1 %all-to-all-start = ((f32[32,1,256]{2,1,0:T(1,128)}), f32[32,1,256]{2,1,0:T(1,128)S(1)}, u32[]{:S(2)}, u32[]{:S(2)}) async-start(f32[32,1,256]{2,1,0:T(1,128)} %reshape.219), calls=%async_computation | async-start | bytes 65536 | tf_op jit(solution)/shard_map/all_to_all | solution.py:32
  85.7 2.4 %fusion.12 = f32[8,8,4,128]{3,2,1,0:T(4,128)S(1)} fusion(f32[8,8,4,128]{3,2,1,0:T(4,128)S(1)} %get-tuple-element.22, f32[8,8,128]{2,1,0:T(8,128)} %copy.60, f32[8,8,4]{2,1,0:T(8,128)S(1)} %convert_element_type.104, f32[8,8,4]{2,1,0:T(8,128)S(1)} %fusion.36, pred[8,128]{1,0:T(8,128)(4,1)S(1)} %fusion.45, bf16[8,128,1024]{2,1,0:T(8,128)(2,1)} %param.20), kind=kOutput, calls=%fused_computation.10 | convolution fusion | flops 8552448 | bytes 2395136 | tf_op jit(solution)/shard_map/bkgw,bwkd->bkgd/dot_general | solution.py:148
  88.1 0.1 copy.66
  88.3 0.1 copy.67
  88.3 7.3 %all-to-all-done = f32[32,1,256]{2,1,0:T(1,128)S(1)} async-done(((f32[32,1,256]{2,1,0:T(1,128)}), f32[32,1,256]{2,1,0:T(1,128)S(1)}, u32[]{:S(2)}, u32[]{:S(2)}) %all-to-all-start) | async-done | bytes 32800 | tf_op jit(solution)/shard_map/all_to_all | solution.py:32
  95.6 0.5 broadcast.177
  96.1 0.7 reduce.1
  96.8 0.1 reshape.220
  97.0 0.1 copy.64
  97.1 0.7 reshape.221
  97.8 3.8 %all-to-all-start.2 = ((f32[32,1,256]{2,1,0:T(1,128)}), f32[32,1,256]{2,1,0:T(1,128)S(1)}, u32[]{:S(2)}, u32[]{:S(2)}) async-start(f32[32,1,256]{2,1,0:T(1,128)} %reshape.221), calls=%async_computation.2 | async-start | bytes 65536 | tf_op jit(solution)/shard_map/all_to_all | solution.py:32
  101.6 0.7 fusion.25
  102.4 9.1 %all-to-all-done.2 = f32[32,1,256]{2,1,0:T(1,128)S(1)} async-done(((f32[32,1,256]{2,1,0:T(1,128)}), f32[32,1,256]{2,1,0:T(1,128)S(1)}, u32[]{:S(2)}, u32[]{:S(2)}) %all-to-all-start.2) | async-done | bytes 32800 | tf_op jit(solution)/shard_map/all_to_all | solution.py:32
  111.5 3.9 %all-to-all-start.1 = ((bf16[32,8,128]{2,1,0:T(8,128)(2,1)}), bf16[32,8,128]{2,1,0:T(8,128)(2,1)S(1)}, u32[]{:S(2)}, u32[]{:S(2)}) async-start(bf16[32,8,128]{2,1,0:T(8,128)(2,1)} %fusion.25), calls=%async_computation.1 | async-start | bytes 131072 | tf_op jit(solution)/shard_map/all_to_all | solution.py:50
  115.3 0.7 reduce.2
  116.1 0.1 reshape.222
  116.2 0.1 copy.68
  116.3 0.1 broadcast_bitcast_fusion
  116.4 9.0 %all-to-all-done.1 = bf16[32,8,128]{2,1,0:T(8,128)(2,1)S(1)} async-done(((bf16[32,8,128]{2,1,0:T(8,128)(2,1)}), bf16[32,8,128]{2,1,0:T(8,128)(2,1)S(1)}, u32[]{:S(2)}, u32[]{:S(2)}) %all-to-all-start.1) | async-done | bytes 65568 | tf_op jit(solution)/shard_map/all_to_all | solution.py:50
  125.4 0.2 fusion.15
  125.6 13.2 %all_to_all.36 = bf16[32,8,128]{2,1,0:T(8,128)(2,1)S(1)} all-to-all(bf16[32,8,128]{2,1,0:T(8,128)(2,1)S(1)} %fusion.15), channel_id=1, replica_groups=mesh['batch'=8,'cache'=32] {'cache'}, dimensions={0} | all-to-all | bytes 131072 | tf_op jit(solution)/shard_map/all_to_all | solution.py:50
  138.8 0.8 fusion.46
  139.6 0.6 broadcast_in_dim.83
  140.2 3.9 %all-to-all-start.4 = ((f32[32,1,8]{2,1,0:T(1,128)}), f32[32,1,8]{2,1,0:T(1,128)S(1)}, u32[]{:S(2)}, u32[]{:S(2)}) async-start(f32[32,1,8]{2,1,0:T(1,128)} %broadcast_in_dim.83), calls=%async_computation.4 | async-start | bytes 32768 | tf_op jit(solution)/shard_map/all_to_all | solution.py:32
  144.1 0.8 dynamic-slice_convert_fusion
  144.8 9.1 %all-to-all-done.4 = f32[32,1,8]{2,1,0:T(1,128)S(1)} async-done(((f32[32,1,8]{2,1,0:T(1,128)}), f32[32,1,8]{2,1,0:T(1,128)S(1)}, u32[]{:S(2)}, u32[]{:S(2)}) %all-to-all-start.4) | async-done | bytes 1056 | tf_op jit(solution)/shard_map/all_to_all | solution.py:32
  153.9 0.1 reduce_sum.78
  154.0 0.1 fusion.48
  154.1 13.0 %all_to_all.37 = bf16[32,8,128]{2,1,0:T(8,128)(2,1)S(1)} all-to-all(bf16[32,8,128]{2,1,0:T(8,128)(2,1)S(1)} %broadcast_in_dim.84), channel_id=1, replica_groups=mesh['batch'=8,'cache'=32] {'cache'}, dimensions={0} | all-to-all | bytes 131072 | tf_op jit(solution)/shard_map/all_to_all | solution.py:32
  167.0 2.1 %fusion.29 = f32[8,224]{1,0:T(8,128)S(1)} fusion(bf16[4096,224]{0,1:T(8,128)(2,1)} %param.25, bf16[32,8,128]{2,1,0:T(8,128)(2,1)S(1)} %all_to_all.37), kind=kOutput, calls=%fused_computation.38 | convolution fusion | flops 14680064 | bytes 1907712 | tf_op jit(solution)/shard_map/dot_general | solution.py:184
  169.1 3.4 %fusion.16 = bf16[32,8,128]{2,1,0:T(8,128)(2,1)S(1)} fusion(bf16[224,4096]{1,0:T(8,128)(2,1)} %param.27, bf16[4096,224]{0,1:T(8,128)(2,1)} %param.26, bf16[32,8,128]{2,1,0:T(8,128)(2,1)S(1)} %all_to_all.37, f32[8,224]{1,0:T(8,128)S(1)} %fusion.29), kind=kOutput, calls=%fused_computation.12 | convolution fusion | flops 29403648 | bytes 3808256 | tf_op jit(solution)/shard_map/dot_general | solution.py:187
  172.5 13.2 %all_to_all.38 = bf16[32,8,128]{2,1,0:T(8,128)(2,1)S(1)} all-to-all(bf16[32,8,128]{2,1,0:T(8,128)(2,1)S(1)} %fusion.16), channel_id=1, replica_groups=mesh['batch'=8,'cache'=32] {'cache'}, dimensions={0} | all-to-all | bytes 131072 | tf_op jit(solution)/shard_map/all_to_all | solution.py:50
  185.7 0.6 fusion.49
  (37 shorter events, 0.4 us)
Async XLA Ops:
  0.0 76.9 %copy-start = (bf16[8,128,1024]{2,1,0:T(8,128)(2,1)S(1)}, bf16[8,128,1024]{2,1,0:T(8,128)(2,1)}, u32[]{:S(2)}) copy-start(bf16[8,128,1024]{2,1,0:T(8,128)(2,1)} %param.19) | copy-start | bytes 6291460
  0.0 54.9 %copy-start.3 = (s32[8]{0:T(128)S(1)}, s32[8]{0:T(128)}, u32[]{:S(2)}) copy-start(s32[8]{0:T(128)} %param.21) | copy-start | bytes 100
  0.0 54.7 %copy-start.2 = (s32[8]{0:T(128)S(1)}, s32[8]{0:T(128)}, u32[]{:S(2)}) copy-start(s32[8]{0:T(128)} %param.22) | copy-start | bytes 100
  3.4 51.5 %collective-permute-start = (bf16[8,128]{1,0:T(8,128)(2,1)S(1)}, bf16[8,128]{1,0:T(8,128)(2,1)S(1)}, u32[]{:S(2)}, u32[]{:S(2)}) collective-permute-start(bf16[8,128]{1,0:T(8,128)(2,1)S(1)} %convolution_convert_fusion.4), channel_id=1, source_target_pairs={{0,1},{1,0},{2,3},{3,2},{4,5},{5,4},{6,7},{7,6},{8,9},{9,8},{10,11... | collective-permute-start | bytes 6152 | tf_op jit(solution)/shard_map/ppermute | solution.py:15
  55.0 4.6 %collective-permute-start.1 = (bf16[8,256]{1,0:T(8,128)(2,1)S(1)}, bf16[8,256]{1,0:T(8,128)(2,1)S(1)}, u32[]{:S(2)}, u32[]{:S(2)}) collective-permute-start(bf16[8,256]{1,0:T(8,128)(2,1)S(1)} %maximum_select_fusion.7), channel_id=1, source_target_pairs={{0,2},{1,3},{2,0},{3,1},{4,6},{5,7},{6,4},{7,5},{8,10},{9,11},{10,... | collective-permute-start | bytes 12296 | tf_op jit(solution)/shard_map/ppermute | solution.py:15
  59.6 7.6 %collective-permute-start.2 = (bf16[8,512]{1,0:T(8,128)(2,1)S(1)}, bf16[8,512]{1,0:T(8,128)(2,1)S(1)}, u32[]{:S(2)}, u32[]{:S(2)}) collective-permute-start(bf16[8,512]{1,0:T(8,128)(2,1)S(1)} %maximum_select_fusion.6), channel_id=1, source_target_pairs={{0,4},{1,5},{2,6},{3,7},{4,0},{5,1},{6,2},{7,3},{8,12},{9,13},{10,... | collective-permute-start | bytes 24584 | tf_op jit(solution)/shard_map/ppermute | solution.py:15
  67.2 3.7 %collective-permute-start.3 = (bf16[8,1024]{1,0:T(8,128)(2,1)S(1)}, bf16[8,1024]{1,0:T(8,128)(2,1)S(1)}, u32[]{:S(2)}, u32[]{:S(2)}) collective-permute-start(bf16[8,1024]{1,0:T(8,128)(2,1)S(1)} %maximum_select_fusion.4), channel_id=1, source_target_pairs={{0,8},{1,9},{2,10},{3,11},{4,12},{5,13},{6,14},{7,15},{8,0},{9,1},... | collective-permute-start | bytes 49160 | tf_op jit(solution)/shard_map/ppermute | solution.py:15
  70.9 5.5 %collective-permute-start.4 = (bf16[8,2048]{1,0:T(8,128)(2,1)S(1)}, bf16[8,2048]{1,0:T(8,128)(2,1)S(1)}, u32[]{:S(2)}, u32[]{:S(2)}) collective-permute-start(bf16[8,2048]{1,0:T(8,128)(2,1)S(1)} %maximum_select_fusion.2), channel_id=1, source_target_pairs={{0,16},{1,17},{2,18},{3,19},{4,20},{5,21},{6,22},{7,23},{8,24},{9,... | collective-permute-start | bytes 98312 | tf_op jit(solution)/shard_map/ppermute | solution.py:15
  79.6 16.0 %all-to-all-start = ((f32[32,1,256]{2,1,0:T(1,128)}), f32[32,1,256]{2,1,0:T(1,128)S(1)}, u32[]{:S(2)}, u32[]{:S(2)}) async-start(f32[32,1,256]{2,1,0:T(1,128)} %reshape.219), calls=%async_computation | async-start | bytes 65536 | tf_op jit(solution)/shard_map/all_to_all | solution.py:32
  85.7 39.6 %copy-start.1 = (bf16[128,4096]{1,0:T(8,128)(2,1)S(1)}, bf16[128,4096]{1,0:T(8,128)(2,1)}, u32[]{:S(2)}) copy-start(bf16[128,4096]{1,0:T(8,128)(2,1)} %param.23) | copy-start | bytes 3145732
  97.8 13.7 %all-to-all-start.2 = ((f32[32,1,256]{2,1,0:T(1,128)}), f32[32,1,256]{2,1,0:T(1,128)S(1)}, u32[]{:S(2)}, u32[]{:S(2)}) async-start(f32[32,1,256]{2,1,0:T(1,128)} %reshape.221), calls=%async_computation.2 | async-start | bytes 65536 | tf_op jit(solution)/shard_map/all_to_all | solution.py:32
  111.5 13.9 %all-to-all-start.1 = ((bf16[32,8,128]{2,1,0:T(8,128)(2,1)}), bf16[32,8,128]{2,1,0:T(8,128)(2,1)S(1)}, u32[]{:S(2)}, u32[]{:S(2)}) async-start(bf16[32,8,128]{2,1,0:T(8,128)(2,1)} %fusion.25), calls=%async_computation.1 | async-start | bytes 131072 | tf_op jit(solution)/shard_map/all_to_all | solution.py:50
  140.2 13.7 %all-to-all-start.4 = ((f32[32,1,8]{2,1,0:T(1,128)}), f32[32,1,8]{2,1,0:T(1,128)S(1)}, u32[]{:S(2)}, u32[]{:S(2)}) async-start(f32[32,1,8]{2,1,0:T(1,128)} %broadcast_in_dim.83), calls=%async_computation.4 | async-start | bytes 32768 | tf_op jit(solution)/shard_map/all_to_all | solution.py:32
